TPU v7x, 32 devices: a whole 2x2x4 slice. The times are simulated.
32 devices in a mesh: dp: 4 (over y, x), expert: 4 (over z), tensor: 2 (over core).
Axes of the slice: x: 2, y: 2, z: 4, core: 2. Of those that a mesh axis runs over, the one named last changes fastest.
Arguments:
- tokens: bfloat16 [1, 256, 3584], P(None, ('dp', 'expert'), 'tensor'), may hold values from -6 to 6
- gate_weight: bfloat16 [16, 3584, 1024], P(('dp', 'expert'), None, 'tensor'), may hold values from -0.09375 to 0.09375
- up_weight: bfloat16 [16, 3584, 1024], P(('dp', 'expert'), None, 'tensor'), may hold values from -0.09375 to 0.09375
- down_weight: bfloat16 [16, 1024, 3584], P(('dp', 'expert'), 'tensor'), may hold values from -0.1875 to 0.1875
- expert_ids: int32 [1, 256, 8], P(None, ('dp', 'expert')), may hold values from 0 to 15, all different within a row; in each aligned block of 16 rows (0 to 15, 16 to 31, ..., all dimensions but the last counted through in order) at most 16 rows name the same one
- gate_codes: int32 [1, 256, 8], P(None, ('dp', 'expert')), may hold values from 1 to 32767
Outputs:
- mixed: bfloat16 [1, 256, 3584], P(None, ('dp', 'expert'), 'tensor')
Inputs may be any that keep to these rules, and one draw needn't show every extreme that they name: `expert_ids`: the 8 experts of one token differ. For every step, of the 16 tokens that one index of dp+expert holds, no expert is named by more than 16.
All inputs are finite; a program needn't handle non-finite values.
Results may differ from a plain program's by a relative error of at most 0.0095.
Values may be sent and summed in bfloat16 or wider, within the bound.
A program may use at most 64 MiB of HBM per device.

v0:
```python
import jax
import jax.numpy as jnp
from jax import lax
from jax.sharding import PartitionSpec as P


def local(tokens, gate_weight, up_weight, down_weight, expert_ids, gate_codes):
    owners = lax.axis_size("dp") * lax.axis_size("expert")
    tok_rows = tokens.shape[1]
    top_count = expert_ids.shape[2]
    slot_depth = min(tok_rows, max(2, 2 * tok_rows * top_count // owners))
    slot_count = owners * slot_depth
    w_gate = gate_weight[0]
    w_up = up_weight[0]
    w_down = down_weight[0]
    slot_numbers = jnp.arange(slot_count, dtype=jnp.int32)
    owner_numbers = jnp.arange(owners, dtype=jnp.int32)
    step_tokens = tokens[0]
    route_ids = expert_ids[0].reshape(tok_rows * top_count)
    onehot = (route_ids[:, None] == owner_numbers[None, :]).astype(jnp.int32)
    before = jnp.cumsum(onehot, axis=0) - onehot
    slot_rank = jnp.sum(before * onehot, axis=1)
    slot_index = route_ids * slot_depth + slot_rank
    select = (slot_index[:, None] == slot_numbers[None, :]).astype(jnp.bfloat16)
    per_token = jnp.sum(select.reshape(tok_rows, top_count, slot_count), axis=1)
    packed = jnp.einsum(
        "ts,td->sd", per_token, step_tokens, preferred_element_type=jnp.float32
    ).astype(jnp.bfloat16)
    packed = packed.reshape(owners, slot_depth, step_tokens.shape[1])
    arrived = lax.all_to_all(packed, ("dp", "expert"), split_axis=0, concat_axis=0, tiled=True)
    owner_rows = arrived.reshape(slot_count, step_tokens.shape[1])
    owner_rows = lax.all_gather(owner_rows, "tensor", axis=1, tiled=True)
    gated = jnp.dot(owner_rows, w_gate, preferred_element_type=jnp.float32)
    lifted = jnp.dot(owner_rows, w_up, preferred_element_type=jnp.float32)
    hidden = (jax.nn.silu(gated) * lifted).astype(jnp.bfloat16)
    partial_value = jnp.dot(hidden, w_down, preferred_element_type=jnp.float32).astype(jnp.bfloat16)
    summed = (
        lax.psum_scatter(partial_value, "tensor", scatter_dimension=1, tiled=True)
        .astype(jnp.float32)
        .astype(jnp.bfloat16)
    )
    half_width = summed.shape[1]
    result = summed.reshape(owners, slot_depth, half_width)
    returned = lax.all_to_all(result, ("dp", "expert"), split_axis=0, concat_axis=0, tiled=True)
    returned = returned.reshape(slot_count, half_width)
    picked = jnp.dot(select, returned, preferred_element_type=jnp.float32)
    codes = gate_codes[0].astype(jnp.float32)
    shares = codes / jnp.sum(codes, axis=1, keepdims=True)
    mixed_rows = jnp.sum(
        picked.reshape(tok_rows, top_count, half_width) * shares[:, :, None], axis=1
    )
    outputs = [mixed_rows.astype(jnp.bfloat16)]
    return jnp.stack(outputs)


def solution(mesh):
    in_specs = (
        P(None, ("dp", "expert"), "tensor"),
        P(("dp", "expert"), None, "tensor"),
        P(("dp", "expert"), None, "tensor"),
        P(("dp", "expert"), "tensor", None),
        P(None, ("dp", "expert"), None),
        P(None, ("dp", "expert"), None),
    )
    out_specs = P(None, ("dp", "expert"), "tensor")
    return jax.shard_map(local, mesh=mesh, in_specs=in_specs, out_specs=out_specs, check_vma=False)
```

profile of v0, /device:TPU:0, one launch (start us, length us, event | category | flops | bytes accessed | tf_op | source)
XLA Modules:
  0.0 110.7 jit_solution(10478560798243014809)
XLA Ops:
  6.5 0.0 copy-start
  6.5 0.0 all-gather.2.cloned.1.call-start
  6.5 0.8 copy.17
  7.3 0.1 eq.51
  7.4 0.1 fusion.25
  7.5 0.2 reduce_window_sum.11
  7.7 0.2 select_reduce_fusion
  7.8 0.1 reduce_sum.42
  7.9 0.1 copy.18
  8.0 0.7 bitcast_add_fusion
  8.7 0.1 copy.19
  8.8 0.1 fusion.23
  8.9 0.0 copy-done
  8.9 0.4 convolution_convert_fusion.1
  9.3 32.9 %all_to_all.10 = bf16[16,16,1792]{2,1,0:T(8,128)(2,1)} all-to-all(bf16[16,16,1792]{2,1,0:T(8,128)(2,1)S(1)} %bitcast.39), channel_id=1, replica_groups=mesh['dp'=4,'expert'=4,'tensor'=2] {'dp','expert'}, dimensions={0} | all-to-all | bytes 1835008 | tf_op jit(solution)/shard_map/all_to_all | solution.py:30
  42.2 0.0 all-gather.2.cloned.1.call-update
  42.2 0.0 reduce-scatter.2.cloned.1.call-start
  42.3 7.5 %all-gather.2.cloned.1.call-done = bf16[256,3584]{1,0:T(8,128)(2,1)} async-done(((bf16[256,1792]{1,0:T(8,128)(2,1)}), bf16[256,3584]{1,0:T(8,128)(2,1)}) %all-gather.2.cloned.1.call-update) | async-done | bytes 1835024 | tf_op jit(solution)/shard_map/all_gather | solution.py:32
  49.8 0.0 copy-start.2
  49.8 3.8 %fusion.3 = f32[256,512]{1,0:T(8,128)S(1)} fusion(bf16[256,3584]{1,0:T(8,128)(2,1)} %all-gather.2.cloned.1.call-done, bf16[1,3584,512]{2,1,0:T(8,128)(2,1)} %param.7), kind=kOutput, calls=%fused_computation.4 | convolution fusion | flops 939524096 | bytes 6029312 | tf_op jit(solution)/shard_map/dot_general | solution.py:33
  53.6 0.0 copy-done.2
  53.7 6.6 %convolution_convert_fusion = bf16[256,3584]{1,0:T(8,128)(2,1)} fusion(bf16[1,512,3584]{2,1,0:T(8,128)(2,1)} %param.9, bf16[256,3584]{1,0:T(8,128)(2,1)S(1)} %copy-done.2, bf16[1,3584,512]{2,1,0:T(8,128)(2,1)} %param.8, f32[256,512]{1,0:T(8,128)S(1)} %fusion.3), kind=kOutput, calls=%fused_computation | convolution fusion | flops 1880752128 | bytes 11534336 | tf_op jit(solution)/shard_map/dot_general | solution.py:36
  60.2 0.0 copy-start.1
  60.2 0.0 reduce-scatter.2.cloned.1.call-update
  60.2 10.6 %reduce-scatter.2.cloned.1.call-done = bf16[256,1792]{1,0:T(8,128)(2,1)} async-done(((bf16[256,3584]{1,0:T(8,128)(2,1)}), bf16[256,1792]{1,0:T(8,128)(2,1)}) %reduce-scatter.2.cloned.1.call-update) | async-done | bytes 917520 | tf_op jit(solution)/shard_map/reduce_scatter | solution.py:38
  70.9 6.9 %all-to-all-start.1 = ((bf16[16,16,1792]{2,1,0:T(8,128)(2,1)}), bf16[16,16,1792]{2,1,0:T(8,128)(2,1)S(1)}, u32[]{:S(2)}, u32[]{:S(2)}) async-start(bf16[16,16,1792]{2,1,0:T(8,128)(2,1)} %bitcast.40), calls=%async_computation.2 | async-start | bytes 1835008 | tf_op jit(solution)/shard_map/all_to_all | solution.py:44
  77.8 0.0 copy-done.1
  77.8 0.1 copy.21
  77.9 24.9 %all-to-all-done.1 = bf16[16,16,1792]{2,1,0:T(8,128)(2,1)S(1)} async-done(((bf16[16,16,1792]{2,1,0:T(8,128)(2,1)}), bf16[16,16,1792]{2,1,0:T(8,128)(2,1)S(1)}, u32[]{:S(2)}, u32[]{:S(2)}) %all-to-all-start.1) | async-done | bytes 917536 | tf_op jit(solution)/shard_map/all_to_all | solution.py:44
  102.8 1.1 fusion.8
  (2 shorter events, 0.0 us)
Async XLA Ops:
  6.5 2.4 %copy-start = (bf16[1,16,1792]{2,1,0:T(8,128)(2,1)S(1)}, bf16[1,16,1792]{2,1,0:T(8,128)(2,1)}, u32[]{:S(2)}) copy-start(bf16[1,16,1792]{2,1,0:T(8,128)(2,1)} %param.6) | copy-start | bytes 172036
  6.5 43.3 %all-gather.2.cloned.1.call-start = ((), (), s32[]{:S(2)}) async-start(), calls=%async_computation.3 | async-start | bytes 2752512 | tf_op jit(solution)/shard_map/all_gather | solution.py:32
  42.2 28.6 %reduce-scatter.2.cloned.1.call-start = ((), (), s32[]{:S(2)}) async-start(), calls=%async_computation.4 | async-start | bytes 2752512 | tf_op jit(solution)/shard_map/reduce_scatter | solution.py:38
  49.8 3.8 %copy-start.2 = (bf16[256,3584]{1,0:T(8,128)(2,1)S(1)}, bf16[256,3584]{1,0:T(8,128)(2,1)}, u32[]{:S(2)}) copy-start(bf16[256,3584]{1,0:T(8,128)(2,1)} %all-gather.2.cloned.1.call-done) | copy-start | bytes 5505028
  60.2 17.6 %copy-start.1 = (s32[1,16,8]{1,2,0:T(8,128)S(1)}, s32[1,16,8]{1,2,0:T(8,128)}, u32[]{:S(2)}) copy-start(s32[1,16,8]{1,2,0:T(8,128)} %param.11) | copy-start | bytes 1540
  70.9 31.9 %all-to-all-start.1 = ((bf16[16,16,1792]{2,1,0:T(8,128)(2,1)}), bf16[16,16,1792]{2,1,0:T(8,128)(2,1)S(1)}, u32[]{:S(2)}, u32[]{:S(2)}) async-start(bf16[16,16,1792]{2,1,0:T(8,128)(2,1)} %bitcast.40), calls=%async_computation.2 | async-start | bytes 1835008 | tf_op jit(solution)/shard_map/all_to_all | solution.py:44
Sparse Core Ops, SparseCore 0:
  42.4 7.3 all-gather.1
  60.4 10.4 reduce-scatter.1
where the time goes:
time: 111 us
  waiting for transfers between devices  43 us (39%)
  blocking collectives  32.9 us (30%)
  between operations  13.5 us (12%)
  matrix products  11.9 us (11%)
  starting transfers between devices  6.97 us (6%)
  other arithmetic  1.28 us (1%)
  local copies, waits for them, and re-layouts  1.18 us (1%)
    all_to_all x1, blocking collectives, local(): lax.all_to_all(packed, ('dp', 'expert'), split_axis=0, concat_axis=0, til...  32.9 us
    all_to_all x1, waiting for transfers between devices, local(): lax.all_to_all(result, ('dp', 'expert'), split_axis=0, concat_axis=0, til...  24.9 us
    reduce_scatter x1, waiting for transfers between devices, local(): lax.psum_scatter(partial_value, 'tensor', scatter_dimension=1, tiled=True)  10.6 us
    all_gather x1, waiting for transfers between devices, local(): owner_rows = lax.all_gather(owner_rows, 'tensor', axis=1, tiled=True)  7.52 us
    all_to_all x1, starting transfers between devices, local(): lax.all_to_all(result, ('dp', 'expert'), split_axis=0, concat_axis=0, til...  6.92 us
    dot_general x1, matrix products, local(): jnp.dot(hidden, w_down, preferred_element_type=jnp.float32)  6.57 us
    dot_general x1, matrix products, local(): gated = jnp.dot(owner_rows, w_gate, preferred_element_type=jnp.float32)  3.82 us
  transfers between devices with their start and end apart: 3, of which 3 were waited for; matrix products, arithmetic and copies ran while one was open for 0% of the time, Pallas kernels for 0%

commit v1 on v0

--- a/solution.py
+++ b/solution.py
@@ -29,7 +29,7 @@
     packed = packed.reshape(owners, slot_depth, step_tokens.shape[1])
     arrived = lax.all_to_all(packed, ("dp", "expert"), split_axis=0, concat_axis=0, tiled=True)
     owner_rows = arrived.reshape(slot_count, step_tokens.shape[1])
-    owner_rows = lax.all_gather(owner_rows, "tensor", axis=1, tiled=True)
+    owner_rows = jnp.concatenate(jax.lax.all_gather(owner_rows, "tensor"), axis=1)
     gated = jnp.dot(owner_rows, w_gate, preferred_element_type=jnp.float32)
     lifted = jnp.dot(owner_rows, w_up, preferred_element_type=jnp.float32)
     hidden = (jax.nn.silu(gated) * lifted).astype(jnp.bfloat16)

time: 111 us -> 113 us (1.018)
  local copies, waits for them, and re-layouts: 1.18 us -> 3.97 us
    all_gather x0 -> x1, local copies, waits for them, and re-layouts: none -> 2.8 us  [local(): jax.lax.all_gather(owner_rows, 'tensor')]
where the time goes in v1:
time: 113 us
  waiting for transfers between devices  43 us (38%)
  blocking collectives  32.9 us (29%)
  between operations  13.5 us (12%)
  matrix products  11.3 us (10%)
  starting transfers between devices  6.95 us (6%)
  local copies, waits for them, and re-layouts  3.97 us (4%)
  other arithmetic  1.28 us (1%)
    all_to_all x1, blocking collectives, local(): lax.all_to_all(packed, ('dp', 'expert'), split_axis=0, concat_axis=0, til...  32.9 us
    all_to_all x1, waiting for transfers between devices, local(): lax.all_to_all(result, ('dp', 'expert'), split_axis=0, concat_axis=0, til...  24.9 us
    reduce_scatter x1, waiting for transfers between devices, local(): lax.psum_scatter(partial_value, 'tensor', scatter_dimension=1, tiled=True)  10.6 us
    all_gather x1, waiting for transfers between devices, local(): jax.lax.all_gather(owner_rows, 'tensor')  7.52 us
    all_to_all x1, starting transfers between devices, local(): lax.all_to_all(result, ('dp', 'expert'), split_axis=0, concat_axis=0, til...  6.9 us
    dot_general x1, matrix products, local(): jnp.dot(hidden, w_down, preferred_element_type=jnp.float32)  6.6 us
    dot_general x1, matrix products, local(): gated = jnp.dot(owner_rows, w_gate, preferred_element_type=jnp.float32)  3.16 us
    all_gather x1, local copies, waits for them, and re-layouts, local(): jax.lax.all_gather(owner_rows, 'tensor')  2.8 us
  transfers between devices with their start and end apart: 3, of which 3 were waited for; matrix products, arithmetic and copies ran while one was open for 0% of the time, Pallas kernels for 0%

profile of v1, /device:TPU:0, one launch (start us, length us, event | category | flops | bytes accessed | tf_op | source)
XLA Modules:
  0.0 112.9 jit_solution(3459338048239512679)
XLA Ops:
  6.5 0.0 copy-start
  6.5 0.0 all-gather.2.cloned.1.call-start
  6.5 0.8 copy.30
  7.3 0.1 eq.51
  7.4 0.1 fusion.25
  7.5 0.2 reduce_window_sum.11
  7.7 0.2 select_reduce_fusion
  7.8 0.1 reduce_sum.42
  7.9 0.1 copy.31
  8.0 0.7 bitcast_add_fusion
  8.7 0.1 copy.32
  8.8 0.1 fusion.23
  8.9 0.0 copy-done
  8.9 0.4 convolution_convert_fusion.1
  9.3 32.9 %all_to_all.10 = bf16[16,16,1792]{2,1,0:T(8,128)(2,1)} all-to-all(bf16[16,16,1792]{2,1,0:T(8,128)(2,1)S(1)} %bitcast.42), channel_id=1, replica_groups=mesh['dp'=4,'expert'=4,'tensor'=2] {'dp','expert'}, dimensions={0} | all-to-all | bytes 1835008 | tf_op jit(solution)/shard_map/all_to_all | solution.py:30
  42.2 0.0 all-gather.2.cloned.1.call-update
  42.2 0.0 reduce-scatter.2.cloned.1.call-start
  42.3 7.5 %all-gather.2.cloned.1.call-done = bf16[2,256,1792]{2,1,0:T(8,128)(2,1)} async-done(((bf16[1,256,1792]{2,1,0:T(8,128)(2,1)}), bf16[2,256,1792]{2,1,0:T(8,128)(2,1)}) %all-gather.2.cloned.1.call-update) | async-done | bytes 1835024 | tf_op jit(solution)/shard_map/all_gather | solution.py:32
  49.8 2.8 %copy.34 = bf16[2,256,1792]{1,2,0:T(8,128)(2,1)S(1)} copy(bf16[2,256,1792]{2,1,0:T(8,128)(2,1)} %all-gather.2.cloned.1.call-done) | data formatting | bytes 3670016 | tf_op jit(solution)/shard_map/all_gather | solution.py:32
  52.6 3.2 %fusion.3 = f32[256,512]{1,0:T(8,128)S(1)} fusion(bf16[256,3584]{0,1:T(8,128)(2,1)S(1)} %bitcast.43, bf16[1,3584,512]{2,1,0:T(8,128)(2,1)} %param.7), kind=kOutput, calls=%fused_computation.4 | convolution fusion | flops 939524096 | bytes 6029312 | tf_op jit(solution)/shard_map/dot_general | solution.py:33
  55.8 6.6 %convolution_convert_fusion = bf16[256,3584]{1,0:T(8,128)(2,1)} fusion(bf16[1,512,3584]{2,1,0:T(8,128)(2,1)} %param.9, bf16[256,3584]{0,1:T(8,128)(2,1)S(1)} %bitcast.44, bf16[1,3584,512]{2,1,0:T(8,128)(2,1)} %param.8, f32[256,512]{1,0:T(8,128)S(1)} %fusion.3), kind=kOutput, calls=%fused_computation | convolution fusion | flops 1880752128 | bytes 11534336 | tf_op jit(solution)/shard_map/dot_general | solution.py:36
  62.4 0.0 copy-start.1
  62.4 0.0 reduce-scatter.2.cloned.1.call-update
  62.4 10.6 %reduce-scatter.2.cloned.1.call-done = bf16[256,1792]{1,0:T(8,128)(2,1)} async-done(((bf16[256,3584]{1,0:T(8,128)(2,1)}), bf16[256,1792]{1,0:T(8,128)(2,1)}) %reduce-scatter.2.cloned.1.call-update) | async-done | bytes 917520 | tf_op jit(solution)/shard_map/reduce_scatter | solution.py:38
  73.0 6.9 %all-to-all-start.1 = ((bf16[16,16,1792]{2,1,0:T(8,128)(2,1)}), bf16[16,16,1792]{2,1,0:T(8,128)(2,1)S(1)}, u32[]{:S(2)}, u32[]{:S(2)}) async-start(bf16[16,16,1792]{2,1,0:T(8,128)(2,1)} %bitcast.45), calls=%async_computation.2 | async-start | bytes 1835008 | tf_op jit(solution)/shard_map/all_to_all | solution.py:44
  80.0 0.0 copy-done.1
  80.0 0.1 copy.35
  80.1 24.9 %all-to-all-done.1 = bf16[16,16,1792]{2,1,0:T(8,128)(2,1)S(1)} async-done(((bf16[16,16,1792]{2,1,0:T(8,128)(2,1)}), bf16[16,16,1792]{2,1,0:T(8,128)(2,1)S(1)}, u32[]{:S(2)}, u32[]{:S(2)}) %all-to-all-start.1) | async-done | bytes 917536 | tf_op jit(solution)/shard_map/all_to_all | solution.py:44
  104.9 1.1 fusion.8
  (2 shorter events, 0.0 us)
Async XLA Ops:
  6.5 2.4 %copy-start = (bf16[1,16,1792]{2,1,0:T(8,128)(2,1)S(1)}, bf16[1,16,1792]{2,1,0:T(8,128)(2,1)}, u32[]{:S(2)}) copy-start(bf16[1,16,1792]{2,1,0:T(8,128)(2,1)} %param.6) | copy-start | bytes 172036
  6.5 43.3 %all-gather.2.cloned.1.call-start = ((), (), s32[]{:S(2)}) async-start(), calls=%async_computation.3 | async-start | bytes 2752512 | tf_op jit(solution)/shard_map/all_gather | solution.py:32
  42.2 30.8 %reduce-scatter.2.cloned.1.call-start = ((), (), s32[]{:S(2)}) async-start(), calls=%async_computation.4 | async-start | bytes 2752512 | tf_op jit(solution)/shard_map/reduce_scatter | solution.py:38
  62.4 17.6 %copy-start.1 = (s32[1,16,8]{1,2,0:T(8,128)S(1)}, s32[1,16,8]{1,2,0:T(8,128)}, u32[]{:S(2)}) copy-start(s32[1,16,8]{1,2,0:T(8,128)} %param.11) | copy-start | bytes 1540
  73.0 31.9 %all-to-all-start.1 = ((bf16[16,16,1792]{2,1,0:T(8,128)(2,1)}), bf16[16,16,1792]{2,1,0:T(8,128)(2,1)S(1)}, u32[]{:S(2)}, u32[]{:S(2)}) async-start(bf16[16,16,1792]{2,1,0:T(8,128)(2,1)} %bitcast.45), calls=%async_computation.2 | async-start | bytes 1835008 | tf_op jit(solution)/shard_map/all_to_all | solution.py:44
Sparse Core Ops, SparseCore 0:
  42.4 7.3 all-gather.1
  62.5 10.4 reduce-scatter.1
